TPU v7x, 512 devices: a whole 4x8x8 slice. The times are simulated.
512 devices in a mesh: rows: 512 (over z, y, x, core).
Axes of the slice: x: 4, y: 8, z: 8, core: 2. Of those that a mesh axis runs over, the one named last changes fastest.
Arguments:
- adj_diag: int32 [8192, 512], P('rows'), may hold values from -2147483648 to 2147483647
- adj_right: int32 [8192, 512], P('rows'), may hold values from -2147483648 to 2147483647
- alive_diag: int32 [8192, 512], P('rows'), may hold values from -2147483648 to 2147483647
- alive_right: int32 [8192, 512], P('rows'), may hold values from -2147483648 to 2147483647
- truss_k: int32 [1], replicated, may hold values from 130 to 193
Outputs:
- support_field: float32 [262144, 1024], P('rows')
- removed_counts: int32 [3], replicated
All inputs are finite; a program needn't handle non-finite values.
Results may differ from a plain program's by a relative error of at most 0.0003.
Values may be sent and summed in bfloat16 or wider, within the bound.
A program may use at most 64 MiB of HBM per device.

v0:
```python
import jax
import jax.numpy as jnp
from jax import lax
from jax.sharding import Mesh
from jax.sharding import PartitionSpec as P

ITERS = 3
ROWS = ("rows_0", "rows_1", "rows_2", "rows_3")


def shifted(array, axis, by):
    count = lax.axis_size(axis)
    return lax.ppermute(array, axis, [(i, (i + by) % count) for i in range(count)])


def over_axes(array, axes):
    for axis in axes:
        array = lax.psum(array, axis)
    return array


def unpack_tile(packed):
    shifts = jnp.arange(32, dtype=jnp.int32)
    tile_bits = packed[:, None, :] >> shifts[None, :, None] & 1
    return tile_bits.reshape(packed.shape[0] * 32, packed.shape[1])


def pack_bits(tile_bits):
    shifts = jnp.arange(32, dtype=jnp.int32)
    sectioned = tile_bits.reshape(tile_bits.shape[0] // 32, 32, tile_bits.shape[1])
    return jnp.sum(sectioned << shifts[None, :, None], axis=1, dtype=jnp.int32)


def within_tile(packed):
    upper_half = jnp.triu(unpack_tile(packed), 1)
    return (upper_half + upper_half.T).astype(jnp.bfloat16)


def across_tile(packed):
    return unpack_tile(packed).astype(jnp.bfloat16)


def pack_across(across):
    return pack_bits(across.astype(jnp.int32))


def fold_within(within):
    width = within.shape[0]
    half = width // 2
    row_ids = lax.broadcasted_iota(jnp.int32, (half, width), 0)
    col_ids = lax.broadcasted_iota(jnp.int32, (half, width), 1)
    flipped = within[half:][::-1, ::-1]
    folded = jnp.where(col_ids > row_ids, within[:half], flipped)
    return pack_bits(folded.astype(jnp.int32))


def unfold_within(packed):
    folded = unpack_tile(packed)
    half = folded.shape[0]
    width = folded.shape[1]
    row_ids = lax.broadcasted_iota(jnp.int32, (half, width), 0)
    col_ids = lax.broadcasted_iota(jnp.int32, (half, width), 1)
    top_rows = jnp.where(col_ids > row_ids, folded, jnp.zeros_like(folded))
    bottom_rows = jnp.where(col_ids < row_ids, folded, jnp.zeros_like(folded))[::-1, ::-1]
    upper_half = jnp.concatenate([top_rows, bottom_rows], axis=0)
    return (upper_half + upper_half.T).astype(jnp.bfloat16)


def support_within(prev_across, within, across):
    inside = lax.dot_general(
        prev_across, prev_across, (((0,), (0,)), ((), ())), preferred_element_type=jnp.float32
    )
    inside = inside + jnp.dot(within, within, preferred_element_type=jnp.float32)
    return inside + lax.dot_general(
        across, across, (((1,), (1,)), ((), ())), preferred_element_type=jnp.float32
    )


def support_across(within, across, next_within):
    between = jnp.dot(within, across, preferred_element_type=jnp.float32)
    return between + jnp.dot(across, next_within, preferred_element_type=jnp.float32)


def keep_edges(support, tile_mask, thresh):
    return jnp.where(support >= thresh, tile_mask, jnp.zeros_like(tile_mask))


def peel(prev_across, within, across, next_within, thresh):
    inside = support_within(prev_across, within, across)
    between = support_across(within, across, next_within)
    return (
        inside,
        between,
        keep_edges(inside, within, thresh),
        keep_edges(between, across, thresh),
    )


def tally(within, new_within, across, new_across):
    removed = jnp.sum((within - new_within).astype(jnp.int32)) // 2
    removed = removed + jnp.sum((across - new_across).astype(jnp.int32))
    return removed


def on_device(adj_diag, adj_right, alive_diag, alive_right, truss_k):
    within = within_tile(adj_diag & alive_diag)
    across_words = adj_right & alive_right
    across = across_tile(across_words)
    thresh = (truss_k[0] - 2).astype(jnp.float32)
    counts = []
    for step in range(ITERS):
        prev_across = across_tile(shifted(pack_across(across), ROWS, 1))
        next_within = unfold_within(shifted(fold_within(within), ROWS, -1))
        inside, between, new_within, new_across = peel(
            prev_across, within, across, next_within, thresh
        )
        counts.append(tally(within, new_within, across, new_across))
        within, across = (new_within, new_across)
    stacked = jnp.stack(counts)
    stacked = over_axes(stacked, ROWS)
    support = jnp.concatenate(
        [inside * within.astype(jnp.float32), between * across.astype(jnp.float32)], axis=1
    )
    return (support, stacked)


def solution(mesh):
    split = Mesh(mesh.devices.reshape(8, 8, 4, 2), ("rows_0", "rows_1", "rows_2", "rows_3"))
    placed = (P(ROWS, None), P(ROWS, None), P(ROWS, None), P(ROWS, None), P())
    return jax.shard_map(
        on_device, mesh=split, in_specs=placed, out_specs=(P(ROWS, None), P()), check_vma=False
    )
```

profile of v0, /device:TPU:1, one launch (start us, length us, event | category | flops | bytes accessed | tf_op | source)
XLA Modules:
  0.0 128.3 jit_solution(3447967203919431901)
XLA Ops:
  0.7 0.8 and.74
  2.4 0.9 rev.18
  3.5 8.7 %collective-permute-start.1 = (s32[8,512]{1,0:T(8,128)S(1)}, s32[8,512]{1,0:T(8,128)S(1)}, u32[]{:S(2)}, u32[]{:S(2)}) collective-permute-start(s32[8,512]{1,0:T(8,128)S(1)} %fusion.25), channel_id=1, source_target_pairs={{0,511},{1,0},{2,1},{3,2},{4,3},{5,4},{6,5},{7,6},{8,7},{9,8},{10,... | collective-permute-start | bytes 49160 | tf_op jit(solution)/shard_map/ppermute | solution.py:13
  12.6 1.9 %collective-permute-start = (s32[16,512]{1,0:T(8,128)S(1)}, s32[16,512]{1,0:T(8,128)S(1)}, u32[]{:S(2)}, u32[]{:S(2)}) collective-permute-start(s32[16,512]{1,0:T(8,128)S(1)} %get-tuple-element.9), channel_id=1, source_target_pairs={{0,1},{1,2},{2,3},{3,4},{4,5},{5,6},{6,7},{7,8},{8,9},{9,10},{10,1... | collective-permute-start | bytes 98312 | tf_op jit(solution)/shard_map/ppermute | solution.py:13
  14.6 1.4 %fusion.47 = f32[512,512]{1,0:T(8,128)} fusion(bf16[512,512]{1,0:T(8,128)(2,1)S(1)} %get-tuple-element.17, bf16[512,512]{1,0:T(8,128)(2,1)S(1)} %get-tuple-element.16), kind=kOutput, calls=%fused_computation.93 | convolution fusion | flops 268435456 | bytes 2097152 | tf_op jit(solution)/shard_map/dot_general | solution.py:80
  17.6 1.1 pad_add_fusion
  18.7 2.6 %copy.8 = s32[512,512]{0,1:T(8,128)} copy(s32[512,512]{1,0:T(8,128)} %pad_add_fusion) | data formatting | bytes 2097152 | tf_op jit(solution)/shard_map/concatenate | solution.py:65
  21.3 2.2 %fusion.8 = (s32[16,512]{1,0:T(8,128)S(1)}, bf16[512,512]{1,0:T(8,128)(2,1)S(1)}) fusion(bf16[512,512]{1,0:T(8,128)(2,1)S(1)} %get-tuple-element.16, f32[]{:T(128)} %bitcast.4, f32[512,512]{1,0:T(8,128)} %fusion.47, s32[512,512]{0,1:T(8,128)} %copy.8, s32[256,512]{1,0:T(8,128)S(1)} %rev.19, s32[256,512]{1,0:T(8,128)S(1)} %get-tuple-element.14), kind=kOutput, calls=%fused_computation.25 | convolution fusion | flops 270786560 | bytes 4227076 | tf_op jit(solution)/shard_map/dot_general | solution.py:81
  23.5 1.9 %collective-permute-start.4 = (s32[16,512]{1,0:T(8,128)S(1)}, s32[16,512]{1,0:T(8,128)S(1)}, u32[]{:S(2)}, u32[]{:S(2)}) collective-permute-start(s32[16,512]{1,0:T(8,128)S(1)} %get-tuple-element.20), channel_id=1, source_target_pairs={{0,1},{1,2},{2,3},{3,4},{4,5},{5,6},{6,7},{7,8},{8,9},{9,10},{10,1... | collective-permute-start | bytes 98312 | tf_op jit(solution)/shard_map/ppermute | solution.py:13
  26.9 0.9 rev.20
  28.0 10.1 %collective-permute-start.2 = (s32[8,512]{1,0:T(8,128)S(1)}, s32[8,512]{1,0:T(8,128)S(1)}, u32[]{:S(2)}, u32[]{:S(2)}) collective-permute-start(s32[8,512]{1,0:T(8,128)S(1)} %fusion.24), channel_id=1, source_target_pairs={{0,511},{1,0},{2,1},{3,2},{4,3},{5,4},{6,5},{7,6},{8,7},{9,8},{10,... | collective-permute-start | bytes 49160 | tf_op jit(solution)/shard_map/ppermute | solution.py:13
  39.6 0.9 rev.22
  40.6 9.1 %collective-permute-start.5 = (s32[8,512]{1,0:T(8,128)S(1)}, s32[8,512]{1,0:T(8,128)S(1)}, u32[]{:S(2)}, u32[]{:S(2)}) collective-permute-start(s32[8,512]{1,0:T(8,128)S(1)} %fusion.23), channel_id=1, source_target_pairs={{0,511},{1,0},{2,1},{3,2},{4,3},{5,4},{6,5},{7,6},{8,7},{9,8},{10,... | collective-permute-start | bytes 49160 | tf_op jit(solution)/shard_map/ppermute | solution.py:13
  49.7 1.4 %fusion.48 = f32[512,512]{1,0:T(8,128)} fusion(bf16[512,512]{1,0:T(8,128)(2,1)S(1)} %fusion.7, bf16[512,512]{1,0:T(8,128)(2,1)S(1)} %get-tuple-element.21), kind=kOutput, calls=%fused_computation.94 | convolution fusion | flops 268435456 | bytes 2097152 | tf_op jit(solution)/shard_map/dot_general | solution.py:80
  51.1 1.4 %fusion.28 = (s32[256,512]{1,0:T(8,128)}, s32[256,512]{1,0:T(8,128)}, s32[256,512]{1,0:T(8,128)}, s32[256,512]{1,0:T(8,128)S(1)}) fusion(s32[8,512]{1,0:T(8,128)S(1)} %collective-permute-done.5, s32[256]{0:T(256)S(1)} %shift_left.64, s32[8,512]{1,0:T(8,128)S(1)} %collective-permute-done.2), kind=kLoop, calls=%fused_computation.69 | loop fusion | flops 1310720 | bytes 2130944 | tf_op jit(solution)/shard_map/jit(_where)/select_n | solution.py:63
  52.5 3.9 %rev.21 = s32[256,512]{1,0:T(8,128)S(1)} reverse(s32[256,512]{1,0:T(8,128)} %get-tuple-element.18), dimensions={0,1} | reverse | bytes 1048576 | tf_op jit(solution)/shard_map/rev | solution.py:64
  56.4 1.1 pad_add_fusion.1
  57.5 2.6 %copy.9 = s32[512,512]{0,1:T(8,128)} copy(s32[512,512]{1,0:T(8,128)} %pad_add_fusion.1) | data formatting | bytes 2097152 | tf_op jit(solution)/shard_map/concatenate | solution.py:65
  60.1 2.4 %fusion.9 = (s32[16,512]{1,0:T(8,128)S(1)}, bf16[512,512]{1,0:T(8,128)(2,1)S(1)}) fusion(bf16[512,512]{1,0:T(8,128)(2,1)S(1)} %get-tuple-element.21, f32[]{:T(128)} %bitcast.4, f32[512,512]{1,0:T(8,128)} %fusion.48, s32[512,512]{0,1:T(8,128)} %copy.9, s32[256,512]{1,0:T(8,128)S(1)} %rev.21, s32[256,512]{1,0:T(8,128)} %copy-done.1), kind=kOutput, calls=%fused_computation.27 | convolution fusion | flops 270786560 | bytes 4227076 | tf_op jit(solution)/shard_map/dot_general | solution.py:81
  62.5 1.9 %collective-permute-start.3 = (s32[16,512]{1,0:T(8,128)S(1)}, s32[16,512]{1,0:T(8,128)S(1)}, u32[]{:S(2)}, u32[]{:S(2)}) collective-permute-start(s32[16,512]{1,0:T(8,128)S(1)} %get-tuple-element.24), channel_id=1, source_target_pairs={{0,1},{1,2},{2,3},{3,4},{4,5},{5,6},{6,7},{7,8},{8,9},{9,10},{10,1... | collective-permute-start | bytes 98312 | tf_op jit(solution)/shard_map/ppermute | solution.py:13
  64.4 3.8 %rev.23 = s32[256,512]{1,0:T(8,128)S(1)} reverse(s32[256,512]{1,0:T(8,128)} %get-tuple-element.11), dimensions={0,1} | reverse | bytes 1048576 | tf_op jit(solution)/shard_map/rev | solution.py:64
  68.2 2.1 %pad_add_fusion.2 = s32[512,512]{1,0:T(8,128)} fusion(s32[256,512]{1,0:T(8,128)S(1)} %rev.23, s32[256,512]{1,0:T(8,128)} %get-tuple-element.10), kind=kLoop, calls=%fused_computation.23 | loop fusion | flops 262144 | bytes 2097152 | tf_op jit(solution)/shard_map/concatenate | solution.py:65
  70.3 2.5 %copy.13 = s32[512,512]{0,1:T(8,128)} copy(s32[512,512]{1,0:T(8,128)} %pad_add_fusion.2) | data formatting | bytes 2097152 | tf_op jit(solution)/shard_map/concatenate | solution.py:65
  74.2 1.5 %convert_multiply_fusion = (f32[512,512]{1,0:T(8,128)}, f32[512,512]{1,0:T(8,128)S(1)}) fusion(bf16[512,512]{1,0:T(8,128)(2,1)S(1)} %get-tuple-element.25, f32[]{:T(128)} %bitcast.4, f32[512,512]{1,0:T(8,128)S(1)} %fusion.49, s32[512,512]{0,1:T(8,128)S(1)} %copy-done.3, s32[256,512]{1,0:T(8,128)S(1)} %rev.23, s32[256,512]{1,0:T(8,128)S(1)} %copy-done), kind=kOutput, calls=%fused_computation.48 | convolution fusion | flops 270532608 | bytes 5767172 | tf_op jit(solution)/shard_map/dot_general | solution.py:81
  75.7 1.5 %convert_reduce_fusion.4 = (s32[]{:T(128)}, s32[]{:T(128)}, s32[]{:T(128)}) fusion(bf16[512,512]{1,0:T(8,128)(2,1)S(1)} %get-tuple-element.21, s32[512]{0:T(512)S(1)} %shift_right_arithmetic.162, s32[16,512]{1,0:T(8,128)S(1)} %and.71, bf16[512,512]{1,0:T(8,128)(2,1)S(1)} %get-tuple-element.25, f32[512,512]{1,0:T(8,128)S(1)} %get-tuple-element.23, f32[]{:T(128)} %bitcast.4), kind=kLoop, calls=%fused_computation.46 | loop fusion | flops 4718589 | bytes 2131984 | tf_op jit(solution)/shard_map/reduce_sum | solution.py:101
  78.1 1.5 %convert_multiply_fusion.1 = (f32[512,512]{1,0:T(8,128)}, f32[512,512]{1,0:T(8,128)S(1)}) fusion(bf16[512,512]{1,0:T(8,128)(2,1)S(1)} %fusion.6, f32[]{:T(128)} %bitcast.4, f32[512,512]{1,0:T(8,128)S(1)} %convolution_add_fusion.2, bf16[512,512]{1,0:T(8,128)(2,1)S(1)} %get-tuple-element.25), kind=kOutput, calls=%fused_computation.49 | convolution fusion | flops 269746176 | bytes 4194308 | tf_op jit(solution)/shard_map/dot_general | solution.py:74
  79.6 1.4 %convert_reduce_fusion.5 = (s32[]{:T(128)}, s32[]{:T(128)}, s32[]{:T(128)}) fusion(bf16[512,512]{1,0:T(8,128)(2,1)S(1)} %get-tuple-element.17, bf16[512,512]{1,0:T(8,128)(2,1)S(1)} %fusion.7, bf16[512,512]{1,0:T(8,128)(2,1)S(1)} %fusion.6, f32[512,512]{1,0:T(8,128)S(1)} %get-tuple-element.27, f32[]{:T(128)} %bitcast.4), kind=kLoop, calls=%fused_computation.47 | loop fusion | flops 2883581 | bytes 2621456 | tf_op jit(solution)/shard_map/reduce_sum | solution.py:100
  90.5 7.0 %psum.28 = s32[3]{0:T(128)S(1)} all-reduce(s32[3]{0:T(128)S(1)} %pad_add_fusion.3), channel_id=1, replica_groups=mesh['rows_0'=8,'rows_1'=8,'rows_2'=4,'rows_3'=2] {'rows_0'}, use_global_device_ids=true, to_apply=%region_12.13 | all-reduce | flops 3 | bytes 24 | tf_op jit(solution)/shard_map/psum | solution.py:18
  97.5 7.0 %psum.29 = s32[3]{0:T(128)S(1)} all-reduce(s32[3]{0:T(128)S(1)} %psum.28), channel_id=1, replica_groups=mesh['rows_0'=8,'rows_1'=8,'rows_2'=4,'rows_3'=2] {'rows_1'}, use_global_device_ids=true, to_apply=%region_13.14 | all-reduce | flops 3 | bytes 24 | tf_op jit(solution)/shard_map/psum | solution.py:18
  104.5 11.6 %psum.30 = s32[3]{0:T(128)S(1)} all-reduce(s32[3]{0:T(128)S(1)} %psum.29), channel_id=1, replica_groups=mesh['rows_0'=8,'rows_1'=8,'rows_2'=4,'rows_3'=2] {'rows_2'}, use_global_device_ids=true, to_apply=%region_14.15 | all-reduce | flops 3 | bytes 24 | tf_op jit(solution)/shard_map/psum | solution.py:18
  116.1 9.4 %psum.31 = s32[3]{0:T(128)} all-reduce(s32[3]{0:T(128)S(1)} %psum.30), channel_id=1, replica_groups=mesh['rows_0'=8,'rows_1'=8,'rows_2'=4,'rows_3'=2] {'rows_3'}, use_global_device_ids=true, to_apply=%region_15.16 | all-reduce | flops 3 | bytes 24 | tf_op jit(solution)/shard_map/psum | solution.py:18
  125.5 2.8 %pad_maximum_fusion = f32[512,1024]{1,0:T(8,128)} fusion(f32[512,512]{1,0:T(8,128)} %get-tuple-element.22, f32[512,512]{1,0:T(8,128)S(1)} %copy-done.2), kind=kLoop, calls=%fused_computation | loop fusion | flops 524288 | bytes 4194304 | tf_op jit(solution)/shard_map/concatenate | solution.py:121
  (45 shorter events, 8.0 us)
Async XLA Ops:
  0.6 1.4 %copy-start.4 = (s32[16,512]{1,0:T(8,128)S(1)}, s32[16,512]{1,0:T(8,128)}, u32[]{:S(2)}) copy-start(s32[16,512]{1,0:T(8,128)} %param.6) | copy-start | bytes 98308
  0.6 1.4 %copy-start.5 = (s32[16,512]{1,0:T(8,128)S(1)}, s32[16,512]{1,0:T(8,128)}, u32[]{:S(2)}) copy-start(s32[16,512]{1,0:T(8,128)} %param.8) | copy-start | bytes 98308
  3.5 13.2 %collective-permute-start.1 = (s32[8,512]{1,0:T(8,128)S(1)}, s32[8,512]{1,0:T(8,128)S(1)}, u32[]{:S(2)}, u32[]{:S(2)}) collective-permute-start(s32[8,512]{1,0:T(8,128)S(1)} %fusion.25), channel_id=1, source_target_pairs={{0,511},{1,0},{2,1},{3,2},{4,3},{5,4},{6,5},{7,6},{8,7},{9,8},{10,... | collective-permute-start | bytes 49160 | tf_op jit(solution)/shard_map/ppermute | solution.py:13
  12.6 12.8 %collective-permute-start = (s32[16,512]{1,0:T(8,128)S(1)}, s32[16,512]{1,0:T(8,128)S(1)}, u32[]{:S(2)}, u32[]{:S(2)}) collective-permute-start(s32[16,512]{1,0:T(8,128)S(1)} %get-tuple-element.9), channel_id=1, source_target_pairs={{0,1},{1,2},{2,3},{3,4},{4,5},{5,6},{6,7},{7,8},{8,9},{9,10},{10,1... | collective-permute-start | bytes 98312 | tf_op jit(solution)/shard_map/ppermute | solution.py:13
  23.5 14.6 %collective-permute-start.4 = (s32[16,512]{1,0:T(8,128)S(1)}, s32[16,512]{1,0:T(8,128)S(1)}, u32[]{:S(2)}, u32[]{:S(2)}) collective-permute-start(s32[16,512]{1,0:T(8,128)S(1)} %get-tuple-element.20), channel_id=1, source_target_pairs={{0,1},{1,2},{2,3},{3,4},{4,5},{5,6},{6,7},{7,8},{8,9},{9,10},{10,1... | collective-permute-start | bytes 98312 | tf_op jit(solution)/shard_map/ppermute | solution.py:13
  28.0 23.1 %collective-permute-start.2 = (s32[8,512]{1,0:T(8,128)S(1)}, s32[8,512]{1,0:T(8,128)S(1)}, u32[]{:S(2)}, u32[]{:S(2)}) collective-permute-start(s32[8,512]{1,0:T(8,128)S(1)} %fusion.24), channel_id=1, source_target_pairs={{0,511},{1,0},{2,1},{3,2},{4,3},{5,4},{6,5},{7,6},{8,7},{9,8},{10,... | collective-permute-start | bytes 49160 | tf_op jit(solution)/shard_map/ppermute | solution.py:13
  40.6 10.5 %collective-permute-start.5 = (s32[8,512]{1,0:T(8,128)S(1)}, s32[8,512]{1,0:T(8,128)S(1)}, u32[]{:S(2)}, u32[]{:S(2)}) collective-permute-start(s32[8,512]{1,0:T(8,128)S(1)} %fusion.23), channel_id=1, source_target_pairs={{0,511},{1,0},{2,1},{3,2},{4,3},{5,4},{6,5},{7,6},{8,7},{9,8},{10,... | collective-permute-start | bytes 49160 | tf_op jit(solution)/shard_map/ppermute | solution.py:13
  52.5 5.0 %copy-start.1 = (s32[256,512]{1,0:T(8,128)}, s32[256,512]{1,0:T(8,128)S(1)}, u32[]{:S(2)}) copy-start(s32[256,512]{1,0:T(8,128)S(1)} %get-tuple-element.19) | copy-start | bytes 1572868
  62.5 14.7 %collective-permute-start.3 = (s32[16,512]{1,0:T(8,128)S(1)}, s32[16,512]{1,0:T(8,128)S(1)}, u32[]{:S(2)}, u32[]{:S(2)}) collective-permute-start(s32[16,512]{1,0:T(8,128)S(1)} %get-tuple-element.24), channel_id=1, source_target_pairs={{0,1},{1,2},{2,3},{3,4},{4,5},{5,6},{6,7},{7,8},{8,9},{9,10},{10,1... | collective-permute-start | bytes 98312 | tf_op jit(solution)/shard_map/ppermute | solution.py:13
  72.8 1.0 copy-start
  72.8 1.4 %copy-start.3 = (s32[512,512]{0,1:T(8,128)S(1)}, s32[512,512]{0,1:T(8,128)}, u32[]{:S(2)}) copy-start(s32[512,512]{0,1:T(8,128)} %copy.13) | copy-start | bytes 3145732
  79.6 45.9 %copy-start.2 = (f32[512,512]{1,0:T(8,128)S(1)}, f32[512,512]{1,0:T(8,128)}, u32[]{:S(2)}) copy-start(f32[512,512]{1,0:T(8,128)} %get-tuple-element.26) | copy-start | bytes 3145732
where the time goes:
time: 129 us; the launch traced here: 128 us
  blocking collectives  35 us (27%)
  starting transfers between devices  33.7 us (26%)
  local copies, waits for them, and re-layouts  20.4 us (16%)
  matrix products  14.6 us (11%)
  other arithmetic  13.6 us (11%)
  between operations  11.1 us (9%)
    psum x4, blocking collectives, over_axes(): array = lax.psum(array, axis)  35 us
    ppermute x6, starting transfers between devices, shifted(): lax.ppermute(array, axis, [(i, (i + by) % count) for i in range(count)])  33.7 us
    rev x3, local copies, waits for them, and re-layouts, unfold_within(): jnp.where(col_ids < row_ids, folded, jnp.zeros_like(folded))[::-1, ::-1]  8.42 us
    concatenate x3, local copies, waits for them, and re-layouts, unfold_within(): upper_half = jnp.concatenate([top_rows, bottom_rows], axis=0)  7.69 us
    dot_general x3, matrix products, support_across(): jnp.dot(across, next_within, preferred_element_type=jnp.float32)  6.13 us
    concatenate x3, other arithmetic, unfold_within(): upper_half = jnp.concatenate([top_rows, bottom_rows], axis=0)  4.27 us
    dot_general x3, matrix products, support_across(): between = jnp.dot(within, across, preferred_element_type=jnp.float32)  3.25 us
    concatenate x1, other arithmetic, on_device(): jnp.concatenate([inside * within.astype(jnp.float32), between * across.as...  2.76 us
  transfers between devices with their start and end apart: 6, of which 0 were waited for; matrix products, arithmetic and copies ran while one was open for 21% of the time, Pallas kernels for 0%

commit v1 on v0

v1 whole, which is shorter than its diff:
```python
import functools

import jax
import jax.numpy as jnp
from jax import lax
from jax.experimental import pallas as pl
from jax.experimental.pallas import tpu as pltpu
from jax.sharding import PartitionSpec as P

MESH = pl.DeviceIdType.MESH
AXIS = "rows"
WORD = 32
STAGES = {512: ((1, 8), (8, 8), (64, 8)), 16: ((1, 4), (4, 4))}
HALO = (1, -1, 2, -2)


def upper_words(words):
    row = lax.broadcasted_iota(jnp.int32, words.shape, 0)
    col = lax.broadcasted_iota(jnp.int32, words.shape, 1)
    ahead = col - WORD * row
    low_bits = (jnp.int32(1) << jnp.clip(ahead, 0, WORD - 1)) - 1
    return words & jnp.where(ahead >= WORD, jnp.int32(-1), low_bits)


def unpack(words_ref, out_ref, dtype):
    width = words_ref.shape[1]
    bit = lax.broadcasted_iota(jnp.int32, (WORD, width), 0)
    for w in range(words_ref.shape[0]):
        bits = (jnp.broadcast_to(words_ref[w : w + 1, :], (WORD, width)) >> bit) & 1
        out_ref[w * WORD : (w + 1) * WORD, :] = bits.astype(jnp.float32).astype(dtype)


def dot(a, b, a_dim, b_dim):
    return lax.dot_general(
        a, b, (((a_dim,), (b_dim,)), ((), ())), preferred_element_type=jnp.float32
    )


def kernel(
    ndev, tile,
    adj_diag, adj_right, alive_diag, alive_right, truss_k,
    support, counts,
    staged, k_smem, mine, near, far, wide, across, slots,
    in_sem, k_sem, send_sem, recv_sem, sum_send, sum_recv,
):
    stages = STAGES[ndev]
    words = tile // WORD
    me = lax.axis_index(AXIS)
    loads = [
        pltpu.make_async_copy(src, staged.at[i], in_sem.at[i])
        for i, src in enumerate((adj_diag, alive_diag, adj_right, alive_right))
    ]
    load_k = pltpu.make_async_copy(truss_k, k_smem, k_sem)
    for load in loads:
        load.start()
    load_k.start()

    def at(offset):
        return lax.rem(me + offset + ndev, ndev)

    partners = [[] for _ in stages]
    for s, (stride, size) in enumerate(stages):
        place = lax.rem(me // stride, size)
        for k in range(1, size):
            partners[s].append(me + (lax.rem(place + k, size) - place) * stride)
    barrier = pltpu.get_barrier_semaphore()
    everyone = [at(o) for o in HALO] + sum(partners, [])
    for device in everyone:
        pl.semaphore_signal(barrier, inc=1, device_id=(device,), device_id_type=MESH)

    for load in loads:
        load.wait()
    mine[:words, :] = upper_words(staged[0] & staged[1])
    mine[words:, :] = staged[2] & staged[3]
    load_k.wait()
    thresh = (k_smem[0] - 2).astype(jnp.float32)

    dtype = wide.dtype

    def build_within(ref, slot):
        unpack(ref, wide.at[slot], dtype)
        upper = wide[slot].astype(jnp.float32)
        wide[slot] = (upper + upper.T).astype(dtype)

    build_within(mine.at[:words], 1)
    unpack(mine.at[words:], across.at[2], dtype)

    pl.semaphore_wait(barrier, len(everyone))
    copies = []
    for i, (offset, src, dst) in enumerate((
        (1, mine, near.at[0]),
        (-1, mine, near.at[1]),
        (2, mine.at[words:], far.at[0]),
        (-2, mine.at[:words], far.at[1]),
    )):
        copies.append(pltpu.make_async_remote_copy(
            src_ref=src, dst_ref=dst, send_sem=send_sem.at[i], recv_sem=recv_sem.at[i],
            device_id=(at(offset),), device_id_type=MESH,
        ))
        copies[-1].start()
    for copy in copies:
        copy.wait()
    build_within(near.at[0, :words], 0)
    unpack(near.at[0, words:], across.at[1], dtype)
    build_within(near.at[1, :words], 2)
    unpack(near.at[1, words:], across.at[3], dtype)
    unpack(far.at[0], across.at[0], dtype)
    build_within(far.at[1], 3)

    block = min(256, tile)
    ones = lambda x: jnp.sum(x, axis=0, keepdims=True)

    def lane_sum(x):
        return jnp.sum(x, axis=0, keepdims=True)

    def step_within(a_prev, w, a, new, final=False, count=False):
        before = after = 0
        for r in range(0, tile, block):
            rows = slice(r, r + block)
            s = dot(wide[w, rows, :], wide[w], 1, 0)
            s += dot(across[a, rows, :], across[a], 1, 1)
            s += dot(across[a_prev, :, rows], across[a_prev], 0, 0)
            old = wide[w, rows, :].astype(jnp.float32)
            kept = jnp.where(s >= thresh, old, 0.0)
            if final:
                support[rows, :tile] = s * kept
            else:
                wide[new, rows, :] = kept.astype(dtype)
            if count:
                before += lane_sum(old)
                after += lane_sum(kept)
        return before, after

    def step_across(w, a, w_next, new, final=False, count=False):
        before = after = 0
        for r in range(0, tile, block):
            rows = slice(r, r + block)
            s = dot(wide[w, rows, :], across[a], 1, 0)
            s += dot(across[a, rows, :], wide[w_next], 1, 0)
            old = across[a, rows, :].astype(jnp.float32)
            kept = jnp.where(s >= thresh, old, 0.0)
            if final:
                support[rows, tile:] = s * kept
            else:
                across[new, rows, :] = kept.astype(dtype)
            if count:
                before += lane_sum(old)
                after += lane_sum(kept)
        return before, after

    lost = []
    for j in range(3):
        b = step_within(j, j, j + 1, 4 + j, count=j == 1)
        c = step_across(j, j + 1, j + 1, 4 + j, count=j == 1)
        if j == 1:
            lost.append((b, c))
    for j in range(2):
        b = step_within(4 + j, 5 + j, 5 + j, 7 + j, count=j == 0)
        c = step_across(4 + j, 4 + j, 5 + j, 7 + j, count=j == 1)
        if j == 0:
            keep_b = b
    lost.append((keep_b, c))
    b = step_within(7, 7, 8, None, final=True, count=True)
    c = step_across(7, 8, 8, None, final=True, count=True)
    lost.append((b, c))

    lane = lax.broadcasted_iota(jnp.int32, (1, 128), 1)
    row = jnp.zeros((1, 128), jnp.int32)
    for i, ((b0, b1), (c0, c1)) in enumerate(lost):
        total = jnp.sum(0.5 * (b0 - b1) + (c0 - c1), axis=1, keepdims=True)
        row = jnp.where(lane == i, total.astype(jnp.int32), row)

    n = 0
    for s, (stride, size) in enumerate(stages):
        slots[s, 0:1, :] = row
        sends = []
        for k in range(1, size):
            sends.append(pltpu.make_async_remote_copy(
                src_ref=slots.at[s, 0:1], dst_ref=slots.at[s, k : k + 1],
                send_sem=sum_send.at[n], recv_sem=sum_recv.at[n],
                device_id=(partners[s][k - 1],), device_id_type=MESH,
            ))
            sends[-1].start()
            n += 1
        for send in sends:
            send.wait()
        row = jnp.sum(slots[s, :size, :], axis=0, keepdims=True)
    counts[...] = jnp.broadcast_to(row, counts.shape)


def on_device(ndev, *args):
    tile = args[0].shape[1]
    words = tile // WORD
    sums = sum(size - 1 for _, size in STAGES[ndev])
    vmem = pl.BlockSpec(memory_space=pltpu.VMEM)
    support, counts = pl.pallas_call(
        functools.partial(kernel, ndev, tile),
        out_shape=(
            jax.ShapeDtypeStruct((tile, 2 * tile), jnp.float32),
            jax.ShapeDtypeStruct((8, 128), jnp.int32),
        ),
        in_specs=[pl.BlockSpec(memory_space=pl.ANY)] * 5,
        out_specs=(vmem, vmem),
        scratch_shapes=[
            pltpu.VMEM((4, words, tile), jnp.int32),
            pltpu.SMEM((1,), jnp.int32),
            pltpu.VMEM((2 * words, tile), jnp.int32),
            pltpu.VMEM((2, 2 * words, tile), jnp.int32),
            pltpu.VMEM((2, words, tile), jnp.int32),
            pltpu.VMEM((9, tile, tile), jnp.bfloat16),
            pltpu.VMEM((9, tile, tile), jnp.bfloat16),
            pltpu.VMEM((len(STAGES[ndev]), 8, 128), jnp.int32),
            pltpu.SemaphoreType.DMA((4,)),
            pltpu.SemaphoreType.DMA,
            pltpu.SemaphoreType.DMA((4,)),
            pltpu.SemaphoreType.DMA((4,)),
            pltpu.SemaphoreType.DMA((sums,)),
            pltpu.SemaphoreType.DMA((sums,)),
        ],
        compiler_params=pltpu.CompilerParams(collective_id=0, has_side_effects=True),
        name="peel",
    )(*args)
    return support, counts[0, :3]


def solution(mesh):
    ndev = mesh.shape[AXIS]
    placed = (P(AXIS, None),) * 4 + (P(),)
    return jax.shard_map(
        functools.partial(on_device, ndev), mesh=mesh, in_specs=placed,
        out_specs=(P(AXIS, None), P()), check_vma=False,
    )
```

time: 129 us -> 47.9 us (0.37)
  the two profiles are of different devices: /device:TPU:1 before, /device:TPU:8 now
where the time goes in v1:
time: 47.9 us; the launch traced here: 47.6 us
  Pallas kernels  42 us (88%)
  local copies, waits for them, and re-layouts  4.34 us (9%)
  between operations  1.29 us (3%)
    pallas_call x1, Pallas kernels, on_device(): pl.pallas_call(functools.partial(kernel, ndev, tile), out_shape=(jax.Shap...  42 us
    unnamed x1, local copies, waits for them, and re-layouts  3.16 us
    squeeze x1, local copies, waits for them, and re-layouts, on_device(): return (support, counts[0, :3])  1.19 us

profile of v1, /device:TPU:8, one launch (start us, length us, event | category | flops | bytes accessed | tf_op | source)
XLA Modules:
  0.0 47.6 jit_solution(17337462495330313812)
XLA Ops:
  1.3 42.0 %peel.1 = (f32[512,1024]{1,0:T(8,128)}, s32[8,128]{1,0:T(8,128)}) custom-call(s32[16,512]{1,0:T(8,128)} %adj_diag.1, s32[16,512]{1,0:T(8,128)} %adj_right.1, s32[16,512]{1,0:T(8,128)} %alive_diag.1, s32[16,512]{1,0:T(8,128)} %alive_right.1, s32[1]{0:T(128)S(6)} %copy.8.truss_k), custom_call_target="tpu_custom_call" | custom-call | tf_op jit(solution)/shard_map/peel/pallas_call | solution.py:196
  43.3 1.2 %slice_bitcast_fusion = s32[3]{0:T(128)} fusion(s32[8,128]{1,0:T(8,128)} %get-tuple-element.5), kind=kLoop, calls=%fused_computation | loop fusion | bytes 24 | tf_op jit(solution)/shard_map/squeeze | solution.py:223
  44.5 3.2 %copy.9 = f32[512,1024]{1,0:T(8,128)} copy(f32[512,1024]{1,0:T(8,128)} %get-tuple-element.8) | data formatting | bytes 4194304
